TPU v7x, 128 devices: a whole 4x4x4 slice. The times are simulated.
128 devices in a mesh: row: 4 (over x), col: 4 (over y_lo, core), layer: 8 (over y_hi, z).
Axes of the slice: x: 4, y: 4 (y_hi: 2, y_lo: 2; y = y_hi * 2 + y_lo), z: 4, core: 2. Of those that a mesh axis runs over, the one named last changes fastest.
Arguments:
- left_factor: float32 [6144, 8192], P('row', 'col'), may hold values from -6 to 6
- right_factor: float32 [8192, 6144], P('row', 'col'), may hold values from -0.0625 to 0.0625
Outputs:
- product: float32 [6144, 6144], P(('row', 'layer'), 'col')
All inputs are finite; a program needn't handle non-finite values.
Results may differ from a plain program's by a relative error of at most 0.000073.
Values sent between devices are 32-bit elements; how exact they have to be, the bound alone decides.
A program may use at most 192 MiB of HBM per device.

v0:
```python
import jax
import jax.numpy as jnp
from jax import lax
from jax.sharding import PartitionSpec as P

K = 8192
STEPS = 2


def broadcast(value, axis, root):
    mine = lax.axis_index(axis) == root
    return lax.psum(jnp.where(mine, value, jnp.zeros_like(value)), axis)


def per_device(left_factor, right_factor):
    block_depth = left_factor.shape[1]
    layers = lax.axis_size("layer")
    depth_index = lax.axis_index("layer")
    panel_width = K // (layers * STEPS)
    per_block = block_depth // panel_width
    group_size = 1
    gathered = []
    for step_index in range(0, STEPS, group_size):
        first_panel = depth_index * STEPS + step_index
        source = first_panel // per_block
        offset = first_panel % per_block * panel_width
        left_piece = lax.dynamic_slice_in_dim(left_factor, offset, group_size * panel_width, 1)
        right_piece = lax.dynamic_slice_in_dim(right_factor, offset, group_size * panel_width, 0)
        fetch_left_panel = broadcast(left_piece, "col", source)
        fetch_right_panel = broadcast(right_piece, "row", source)
        gathered.append((fetch_left_panel, fetch_right_panel))
    total = jnp.zeros((left_factor.shape[0], right_factor.shape[1]), jnp.float32)
    for left_panel, right_panel in gathered:
        total = total + jnp.dot(
            left_panel,
            right_panel,
            precision=lax.Precision.HIGHEST,
            preferred_element_type=jnp.float32,
        )
    return lax.psum_scatter(total, "layer", scatter_dimension=0, tiled=True)


def solution(mesh):
    placed = (P("row", "col"), P("row", "col"))
    return jax.shard_map(
        per_device,
        mesh=mesh,
        in_specs=placed,
        out_specs=P(("row", "layer"), "col"),
        check_vma=False,
    )
```

profile of v0, /device:TPU:0, one launch (start us, length us, event | category | flops | bytes accessed | tf_op | source)
XLA Modules:
  0.0 438.1 jit_solution(5593754253861912896)
XLA Ops:
  6.5 0.0 all-reduce.5.cloned.1.call-start
  6.5 6.3 %dynamic-slice_select_fusion.1 = (f32[1536,512]{1,0:T(8,128)}, f32[1536,512]{1,0:T(8,128)}) fusion(f32[1536,2048]{1,0:T(8,128)} %param.2, s32[]{:T(128)S(6)} %select_n.64, pred[]{:T(512)S(6)} %eq.17, s32[]{:T(128)S(6)} %select_n.57, pred[]{:T(512)S(6)} %eq.15), kind=kLoop, calls=%fused_computation.2 | loop fusion | flops 1572864 | bytes 12582922 | tf_op jit(solution)/shard_map/jit(_where)/select_n | solution.py:12
  12.8 0.0 all-reduce.5.cloned.1.call-update
  12.9 0.0 all-reduce.7.cloned.1.call-start
  12.9 6.1 %dynamic-slice_select_fusion = (f32[512,1536]{1,0:T(8,128)}, f32[512,1536]{1,0:T(8,128)}) fusion(f32[2048,1536]{1,0:T(8,128)} %param.3, s32[]{:T(128)S(6)} %select_n.64, pred[]{:T(512)S(6)} %eq.18, s32[]{:T(128)S(6)} %select_n.57, pred[]{:T(512)S(6)} %eq.16), kind=kLoop, calls=%fused_computation.1 | loop fusion | flops 1572864 | bytes 12582922 | tf_op jit(solution)/shard_map/jit(_where)/select_n | solution.py:12
  19.0 0.0 all-reduce.7.cloned.1.call-update
  19.1 0.0 reduce-scatter.2.cloned.1.call-start
  19.1 121.6 %all-reduce.5.cloned.1.call-done = (f32[1536,512]{1,0:T(8,128)}, f32[1536,512]{1,0:T(8,128)}) async-done(((f32[1536,512]{1,0:T(8,128)}, f32[1536,512]{1,0:T(8,128)}), (f32[1536,512]{1,0:T(8,128)}, f32[1536,512]{1,0:T(8,128)})) %all-reduce.5.cloned.1.call-update) | async-done | bytes 6291472 | tf_op jit(solution)/shard_map/psum | solution.py:12
  140.7 130.3 %all-reduce.7.cloned.1.call-done = (f32[512,1536]{1,0:T(8,128)}, f32[512,1536]{1,0:T(8,128)}) async-done(((f32[512,1536]{1,0:T(8,128)}, f32[512,1536]{1,0:T(8,128)}), (f32[512,1536]{1,0:T(8,128)}, f32[512,1536]{1,0:T(8,128)})) %all-reduce.7.cloned.1.call-update) | async-done | bytes 6291472 | tf_op jit(solution)/shard_map/psum | solution.py:12
  271.1 0.0 copy-start
  271.1 0.0 copy-start.1
  271.1 19.7 %fusion = f32[1536,1536]{1,0:T(8,128)S(1)} fusion(f32[1536,512]{1,0:T(8,128)} %get-tuple-element.5, f32[512,1536]{1,0:T(8,128)} %get-tuple-element.7), kind=kOutput, calls=%fused_computation.5 | convolution fusion | flops 14495514624 | bytes 15728640 | tf_op jit(solution)/shard_map/dot_general | solution.py:34
  290.8 0.0 copy-done
  290.8 0.0 copy-done.1
  290.8 18.6 %convolution_add_fusion = f32[1536,1536]{1,0:T(8,128)} fusion(f32[1536,1536]{1,0:T(8,128)S(1)} %fusion, f32[1536,512]{1,0:T(8,128)S(1)} %copy-done, f32[512,1536]{1,0:T(8,128)S(1)} %copy-done.1), kind=kOutput, calls=%fused_computation | convolution fusion | flops 14497873920 | bytes 25165824 | tf_op jit(solution)/shard_map/dot_general | solution.py:34
  309.3 0.0 reduce-scatter.2.cloned.1.call-update
  309.3 122.3 %reduce-scatter.2.cloned.1.call-done = f32[192,1536]{1,0:T(8,128)} async-done(((f32[1536,1536]{1,0:T(8,128)}), f32[192,1536]{1,0:T(8,128)}) %reduce-scatter.2.cloned.1.call-update) | async-done | bytes 1179664 | tf_op jit(solution)/shard_map/reduce_scatter | solution.py:40
Async XLA Ops:
  6.5 134.2 %all-reduce.5.cloned.1.call-start = ((), (), s32[]{:S(2)}) async-start(), calls=%async_computation.2 | async-start | bytes 12582912 | tf_op jit(solution)/shard_map/psum | solution.py:12
  12.9 258.2 %all-reduce.7.cloned.1.call-start = ((), (), s32[]{:S(2)}) async-start(), calls=%async_computation.3 | async-start | bytes 12582912 | tf_op jit(solution)/shard_map/psum | solution.py:12
  19.1 412.5 %reduce-scatter.2.cloned.1.call-start = ((), (), s32[]{:S(2)}) async-start(), calls=%async_computation.1 | async-start | bytes 10616832 | tf_op jit(solution)/shard_map/reduce_scatter | solution.py:40
  271.1 19.7 %copy-start = (f32[1536,512]{1,0:T(8,128)S(1)}, f32[1536,512]{1,0:T(8,128)}, u32[]{:S(2)}) copy-start(f32[1536,512]{1,0:T(8,128)} %get-tuple-element.6) | copy-start | bytes 9437188
  271.1 19.7 %copy-start.1 = (f32[512,1536]{1,0:T(8,128)S(1)}, f32[512,1536]{1,0:T(8,128)}, u32[]{:S(2)}) copy-start(f32[512,1536]{1,0:T(8,128)} %get-tuple-element.8) | copy-start | bytes 9437188
Sparse Core Ops, SparseCore 0:
  13.0 127.6 all-reduce.4
  143.1 127.9 all-reduce.6
  309.5 122.1 reduce-scatter.1
where the time goes:
time: 438 us
  waiting for transfers between devices  374 us (85%)
  matrix products  38.2 us (9%)
  between operations  13.1 us (3%)
  other arithmetic  12.4 us (3%)
    psum x2, waiting for transfers between devices, broadcast(): return lax.psum(jnp.where(mine, value, jnp.zeros_like(value)), axis)  252 us
    reduce_scatter x1, waiting for transfers between devices, per_device(): return lax.psum_scatter(total, 'layer', scatter_dimension=0, tiled=True)  122 us
    dot_general x2, matrix products, per_device(): jnp.dot(left_panel, right_panel, precision=lax.Precision.HIGHEST, preferr...  38.2 us
    select_n x2, other arithmetic, broadcast(): return lax.psum(jnp.where(mine, value, jnp.zeros_like(value)), axis)  12.4 us
  transfers between devices with their start and end apart: 3, of which 3 were waited for; matrix products, arithmetic and copies ran while one was open for 1% of the time, Pallas kernels for 0%

commit v1 on v0

--- a/solution.py
+++ b/solution.py
@@ -2,6 +2,7 @@
 import jax.numpy as jnp
 from jax import lax
 from jax.sharding import PartitionSpec as P
+from jax.lax import all_gather
 
 K = 8192
 STEPS = 2
@@ -9,7 +10,11 @@
 
 def broadcast(value, axis, root):
     mine = lax.axis_index(axis) == root
-    return lax.psum(jnp.where(mine, value, jnp.zeros_like(value)), axis)
+
+    def manage_field_in(message):
+        return all_gather(message, axis).sum(axis=0)
+
+    return manage_field_in(jnp.where(mine, value, jnp.zeros_like(value)))
 
 
 def per_device(left_factor, right_factor):

time: 438 us -> 669 us (1.53)
  waiting for transfers between devices: 374 us -> 574 us
  other arithmetic: 12.4 us -> 42.9 us
    all_gather x0 -> x4, waiting for transfers between devices: none -> 450 us  [manage_field_in(): return all_gather(message, axis).sum(axis=0)]
    psum x2 -> x0, waiting for transfers between devices: 252 us -> none  [broadcast(): return lax.psum(jnp.where(mine, value, jnp.zeros_like(value)), axis)]
    reduce_sum x0 -> x4, other arithmetic: none -> 30.6 us  [manage_field_in(): return all_gather(message, axis).sum(axis=0)]
  transfers between devices with their start and end apart: 3 -> 5, of which waited for: 3 -> 5; matrix products, arithmetic and copies ran while one was open for 1% -> 4% of each run, Pallas kernels for 0% -> 0%
where the time goes in v1:
time: 669 us
  waiting for transfers between devices  574 us (86%)
  other arithmetic  42.9 us (6%)
  matrix products  38.4 us (6%)
  between operations  13.2 us (2%)
    all_gather x4, waiting for transfers between devices, manage_field_in(): return all_gather(message, axis).sum(axis=0)  450 us
    reduce_scatter x1, waiting for transfers between devices, per_device(): return lax.psum_scatter(total, 'layer', scatter_dimension=0, tiled=True)  123 us
    dot_general x2, matrix products, per_device(): jnp.dot(left_panel, right_panel, precision=lax.Precision.HIGHEST, preferr...  38.4 us
    reduce_sum x4, other arithmetic, manage_field_in(): return all_gather(message, axis).sum(axis=0)  30.6 us
  transfers between devices with their start and end apart: 5, of which 5 were waited for; matrix products, arithmetic and copies ran while one was open for 4% of the time, Pallas kernels for 0%

profile of v1, /device:TPU:0, one launch (start us, length us, event | category | flops | bytes accessed | tf_op | source)
XLA Modules:
  0.0 668.8 jit_solution(249793192000669475)
XLA Ops:
  6.5 0.0 all-gather.13.cloned.1.call-start
  6.5 6.2 dynamic-slice_select_fusion.1
  12.7 0.0 all-gather.13.cloned.1.call-update
  12.8 0.0 all-gather.9.cloned.1.call-start
  12.8 0.7 all-gather.9.cloned.1.call-update
  13.5 0.0 all-gather.15.cloned.1.call-start
  13.6 6.1 dynamic-slice_select_fusion
  19.7 0.0 all-gather.15.cloned.1.call-update
  19.7 0.0 all-gather.11.cloned.1.call-start
  19.7 0.5 all-gather.11.cloned.1.call-update
  20.3 0.0 reduce-scatter.2.cloned.1.call-start
  20.3 109.4 %all-gather.13.cloned.1.call-done = f32[6144,512]{1,0:T(8,128)} async-done(((f32[1536,512]{1,0:T(8,128)}), f32[6144,512]{1,0:T(8,128)}) %all-gather.13.cloned.1.call-update) | async-done | bytes 12582928 | tf_op jit(solution)/shard_map/all_gather | solution.py:15
  129.7 6.5 reduce_sum.38
  136.2 112.3 %all-gather.9.cloned.1.call-done = f32[6144,512]{1,0:T(8,128)} async-done(((f32[1536,512]{1,0:T(8,128)}), f32[6144,512]{1,0:T(8,128)}) %all-gather.9.cloned.1.call-update) | async-done | bytes 12582928 | tf_op jit(solution)/shard_map/all_gather | solution.py:15
  248.5 8.1 %reduce_sum.36 = f32[1536,512]{1,0:T(8,128)} reduce(f32[4,1536,512]{2,1,0:T(8,128)} %bitcast.9, f32[]{:T(128)} %constant.58.clone.1), dimensions={0}, to_apply=%region_0.1 | reduce | flops 2359296 | bytes 15728644 | tf_op jit(solution)/shard_map/reduce_sum | solution.py:15
  256.7 114.9 %all-gather.15.cloned.1.call-done = f32[2048,1536]{1,0:T(8,128)} async-done(((f32[512,1536]{1,0:T(8,128)}), f32[2048,1536]{1,0:T(8,128)}) %all-gather.15.cloned.1.call-update) | async-done | bytes 12582928 | tf_op jit(solution)/shard_map/all_gather | solution.py:15
  371.5 8.0 %reduce_sum.39 = f32[512,1536]{1,0:T(8,128)} reduce(f32[4,512,1536]{2,1,0:T(8,128)} %bitcast.10, f32[]{:T(128)} %constant.58.clone.1), dimensions={0}, to_apply=%region_3.4 | reduce | flops 2359296 | bytes 15728644 | tf_op jit(solution)/shard_map/reduce_sum | solution.py:15
  379.5 113.1 %all-gather.11.cloned.1.call-done = f32[2048,1536]{1,0:T(8,128)} async-done(((f32[512,1536]{1,0:T(8,128)}), f32[2048,1536]{1,0:T(8,128)}) %all-gather.11.cloned.1.call-update) | async-done | bytes 12582928 | tf_op jit(solution)/shard_map/all_gather | solution.py:15
  492.6 8.0 %reduce_sum.37 = f32[512,1536]{1,0:T(8,128)} reduce(f32[4,512,1536]{2,1,0:T(8,128)} %bitcast.11, f32[]{:T(128)} %constant.58.clone.1), dimensions={0}, to_apply=%region_1.2 | reduce | flops 2359296 | bytes 15728644 | tf_op jit(solution)/shard_map/reduce_sum | solution.py:15
  500.6 0.0 copy-start
  500.6 19.7 %fusion = f32[1536,1536]{1,0:T(8,128)S(1)} fusion(f32[1536,512]{1,0:T(8,128)} %reduce_sum.36, f32[512,1536]{1,0:T(8,128)} %reduce_sum.37), kind=kOutput, calls=%fused_computation.5 | convolution fusion | flops 14495514624 | bytes 15728640 | tf_op jit(solution)/shard_map/dot_general | solution.py:39
  520.3 0.0 copy-done
  520.3 18.7 %convolution_add_fusion = f32[1536,1536]{1,0:T(8,128)} fusion(f32[1536,1536]{1,0:T(8,128)S(1)} %fusion, f32[1536,512]{1,0:T(8,128)S(1)} %reduce_sum.38, f32[512,1536]{1,0:T(8,128)S(1)} %copy-done), kind=kOutput, calls=%fused_computation | convolution fusion | flops 14497873920 | bytes 25165824 | tf_op jit(solution)/shard_map/dot_general | solution.py:39
  539.0 0.0 reduce-scatter.2.cloned.1.call-update
  539.0 123.2 %reduce-scatter.2.cloned.1.call-done = f32[192,1536]{1,0:T(8,128)} async-done(((f32[1536,1536]{1,0:T(8,128)}), f32[192,1536]{1,0:T(8,128)}) %reduce-scatter.2.cloned.1.call-update) | async-done | bytes 1179664 | tf_op jit(solution)/shard_map/reduce_scatter | solution.py:45
Async XLA Ops:
  6.5 123.2 %all-gather.13.cloned.1.call-start = ((), (), s32[]{:S(2)}) async-start(), calls=%async_computation.4 | async-start | bytes 15728640 | tf_op jit(solution)/shard_map/all_gather | solution.py:15
  12.8 235.8 %all-gather.9.cloned.1.call-start = ((), (), s32[]{:S(2)}) async-start(), calls=%async_computation.2 | async-start | bytes 15728640 | tf_op jit(solution)/shard_map/all_gather | solution.py:15
  13.5 358.0 %all-gather.15.cloned.1.call-start = ((), (), s32[]{:S(2)}) async-start(), calls=%async_computation.5 | async-start | bytes 15728640 | tf_op jit(solution)/shard_map/all_gather | solution.py:15
  19.7 472.9 %all-gather.11.cloned.1.call-start = ((), (), s32[]{:S(2)}) async-start(), calls=%async_computation.3 | async-start | bytes 15728640 | tf_op jit(solution)/shard_map/all_gather | solution.py:15
  20.3 642.0 %reduce-scatter.2.cloned.1.call-start = ((), (), s32[]{:S(2)}) async-start(), calls=%async_computation.1 | async-start | bytes 10616832 | tf_op jit(solution)/shard_map/reduce_scatter | solution.py:45
  500.6 19.7 %copy-start = (f32[512,1536]{1,0:T(8,128)S(1)}, f32[512,1536]{1,0:T(8,128)}, u32[]{:S(2)}) copy-start(f32[512,1536]{1,0:T(8,128)} %reduce_sum.39) | copy-start | bytes 9437188
Sparse Core Ops, SparseCore 0:
  12.9 116.7 all-gather.12
  131.4 117.1 all-gather.8
  250.2 121.3 all-gather.14
  373.0 119.4 all-gather.10
  539.2 123.0 reduce-scatter.1
